TPU v7x, 32 devices: a whole 2x2x4 slice. The times are simulated.
32 devices in a mesh: row: 8 (over z, core), col: 4 (over y, x).
Axes of the slice: x: 2, y: 2, z: 4, core: 2. Of those that a mesh axis runs over, the one named last changes fastest.
Arguments:
- factor: bfloat16 [8192, 8192], P('row', 'col'), as said below
- sel_tiles: int32 [32], replicated, may hold values from 0 to 63, as said below
- coupling: bfloat16 [8192, 2048], P('col', 'row')
Outputs:
- root_inverse: float32 [8192, 8192], P('row', 'col')
- child_inverse: float32 [2048, 8192], P('col', 'row')
Inputs may be any that keep to these rules, and one draw needn't show every extreme that they name: sel_tiles holds 32 distinct tile indices in increasing order; rows of coupling outside the listed tiles are zero. factor is lower triangular with a diagonal between 1 and 1.5.
All inputs are finite; a program needn't handle non-finite values.
Results may differ from a plain program's by a relative error of at most 0.003.
Values may be sent and summed in bfloat16 or wider, within the bound.
A program may use at most 128 MiB of HBM per device.

v0:
```python
import jax
import jax.numpy as jnp
from jax import lax
from jax.sharding import PartitionSpec as P

TILE = 128


def from_root(value, axis, source):
    kept = jnp.where(lax.axis_index(axis) == source, value, 0).astype(value.dtype)
    return lax.psum(kept, axis)


def body(factor, sel_tiles, coupling):
    rows_here = factor.shape[0]
    row_index = lax.axis_index("row")
    whole = lax.all_gather(factor, "row", axis=0, tiled=True)
    ratio = lax.axis_size("row") // lax.axis_size("col")
    offset = row_index % ratio * rows_here
    piece = lax.dynamic_slice_in_dim(whole, offset, rows_here, 1)
    partner = from_root(piece, "col", row_index // ratio)
    gram = lax.dot_general(
        partner, whole, (((0,), (0,)), ((), ())), preferred_element_type=jnp.float32
    )
    coupling_full = lax.all_gather(coupling, "row", axis=1, tiled=True)
    rounded = gram.astype(jnp.bfloat16)
    global_rows = row_index * rows_here + jnp.arange(rows_here, dtype=jnp.int32)
    member = jnp.any((global_rows // TILE)[:, None] == sel_tiles[None, :], axis=1)
    summed = lax.psum_scatter(
        lax.dot_general(
            coupling_full, rounded, (((0,), (1,)), ((), ())), preferred_element_type=jnp.float32
        ),
        "col",
        scatter_dimension=0,
        tiled=True,
    )
    child = jnp.where(member[None, :], -summed, jnp.float32(0.0))
    return (gram, child)


def solution(mesh):
    placed = (P("row", "col"), P(), P("col", "row"))
    return jax.shard_map(
        body,
        mesh=mesh,
        in_specs=placed,
        out_specs=(P("row", "col"), P("col", "row")),
        check_vma=False,
    )
```

profile of v0, /device:TPU:0, one launch (start us, length us, event | category | flops | bytes accessed | tf_op | source)
XLA Modules:
  0.0 817.3 jit_solution(11417977400386051904)
XLA Ops:
  7.2 0.0 all-gather.3.cloned.1.call-start
  7.2 0.7 all-gather.3.cloned.1.call-update
  7.9 0.0 all-reduce.2.cloned.1.call-start
  8.0 293.0 %all-gather.3.cloned.1.call-done = bf16[8192,2048]{1,0:T(8,128)(2,1)} async-done(((bf16[1024,2048]{1,0:T(8,128)(2,1)}), bf16[8192,2048]{1,0:T(8,128)(2,1)}) %all-gather.3.cloned.1.call-update) | async-done | bytes 33554448 | tf_op jit(solution)/shard_map/all_gather | solution.py:17
  300.9 15.0 %dynamic-slice_select_fusion = bf16[8192,1024]{1,0:T(8,128)(2,1)} fusion(bf16[8192,2048]{1,0:T(8,128)(2,1)} %all-gather.3.cloned.1.call-done, s32[]{:T(128)S(6)} %select_n.38, pred[]{:T(512)S(6)} %eq.18), kind=kLoop, calls=%fused_computation | loop fusion | flops 8388608 | bytes 33554436 | tf_op jit(solution)/shard_map/jit(_where)/select_n | solution.py:10
  316.0 0.0 all-reduce.2.cloned.1.call-update
  316.0 0.0 all-gather.5.cloned.1.call-start
  316.0 0.7 all-gather.5.cloned.1.call-update
  316.7 0.0 reduce-scatter.2.cloned.1.call-start
  316.8 304.9 %all-reduce.2.cloned.1.call-done = bf16[8192,1024]{1,0:T(8,128)(2,1)} async-done(((bf16[8192,1024]{1,0:T(8,128)(2,1)}), bf16[8192,1024]{1,0:T(8,128)(2,1)}) %all-reduce.2.cloned.1.call-update) | async-done | bytes 16777232 | tf_op jit(solution)/shard_map/psum | solution.py:11
  621.7 43.9 %fusion.4 = f32[1024,2048]{1,0:T(8,128)} fusion(bf16[8192,1024]{1,0:T(8,128)(2,1)} %all-reduce.2.cloned.1.call-done, bf16[8192,2048]{1,0:T(8,128)(2,1)} %all-gather.3.cloned.1.call-done), kind=kOutput, calls=%fused_computation.14 | convolution fusion | flops 34359738368 | bytes 58720256 | tf_op jit(solution)/shard_map/dot_general | solution.py:22
  665.6 41.2 %all-gather.5.cloned.1.call-done = bf16[2048,2048]{1,0:T(8,128)(2,1)} async-done(((bf16[2048,256]{1,0:T(8,128)(2,1)}), bf16[2048,2048]{1,0:T(8,128)(2,1)}) %all-gather.5.cloned.1.call-update) | async-done | bytes 8388624 | tf_op jit(solution)/shard_map/all_gather | solution.py:25
  706.8 15.6 %convolution_bitcast_fusion = f32[2048,1024]{0,1:T(8,128)} fusion(bf16[2048,2048]{1,0:T(8,128)(2,1)} %all-gather.5.cloned.1.call-done, f32[1024,2048]{1,0:T(8,128)} %fusion.4), kind=kOutput, calls=%fused_computation.1 | convolution fusion | flops 8592031744 | bytes 25165824 | tf_op jit(solution)/shard_map/dot_general | solution.py:30
  722.4 0.0 copy-start
  722.4 0.0 reduce-scatter.2.cloned.1.call-update
  722.5 0.6 copy-done
  723.1 0.1 compare_reduce_fusion
  723.2 83.9 %reduce-scatter.2.cloned.1.call-done = f32[512,1024]{0,1:T(8,128)} async-done(((f32[2048,1024]{0,1:T(8,128)}), f32[512,1024]{0,1:T(8,128)}) %reduce-scatter.2.cloned.1.call-update) | async-done | bytes 2097168 | tf_op jit(solution)/shard_map/reduce_scatter | solution.py:29
  807.1 1.9 negate_select_fusion
  809.0 1.8 copy.6
  (1 shorter events, 0.0 us)
Async XLA Ops:
  7.2 293.8 %all-gather.3.cloned.1.call-start = ((), (), s32[]{:S(2)}) async-start(), calls=%async_computation.1 | async-start | bytes 37748736 | tf_op jit(solution)/shard_map/all_gather | solution.py:17
  7.9 613.8 %all-reduce.2.cloned.1.call-start = ((), (), s32[]{:S(2)}) async-start(), calls=%async_computation.2 | async-start | bytes 33554432 | tf_op jit(solution)/shard_map/psum | solution.py:11
  316.0 390.8 %all-gather.5.cloned.1.call-start = ((), (), s32[]{:S(2)}) async-start(), calls=%async_computation.3 | async-start | bytes 9437184 | tf_op jit(solution)/shard_map/all_gather | solution.py:25
  316.7 490.4 %reduce-scatter.2.cloned.1.call-start = ((), (), s32[]{:S(2)}) async-start(), calls=%async_computation.4 | async-start | bytes 10485760 | tf_op jit(solution)/shard_map/reduce_scatter | solution.py:29
  722.4 0.7 copy-start
Sparse Core Ops, SparseCore 0:
  9.6 291.3 all-gather.2
  316.1 305.5 all-reduce.1
  623.3 83.5 all-gather.4
  722.6 84.4 reduce-scatter.1
where the time goes:
time: 818 us; the launch traced here: 817 us
  waiting for transfers between devices  724 us (89%)
  matrix products  59.6 us (7%)
  other arithmetic  17 us (2%)
  between operations  13.8 us (2%)
    psum x1, waiting for transfers between devices, from_root(): return lax.psum(kept, axis)  305 us
    all_gather x1, waiting for transfers between devices, body(): whole = lax.all_gather(factor, 'row', axis=0, tiled=True)  293 us
    reduce_scatter x1, waiting for transfers between devices, body(): lax.psum_scatter(lax.dot_general(coupling_full, rounded, (((0,), (1,)), (...  83.9 us
    dot_general x1, matrix products, body(): lax.dot_general(partner, whole, (((0,), (0,)), ((), ())), preferred_eleme...  43.9 us
    all_gather x1, waiting for transfers between devices, body(): coupling_full = lax.all_gather(coupling, 'row', axis=1, tiled=True)  41.2 us
  transfers between devices with their start and end apart: 4, of which 4 were waited for; matrix products, arithmetic and copies ran while one was open for 5% of the time, Pallas kernels for 0%

commit v1 on v0

v1 whole, which is shorter than its diff:
```python
import functools
import math

import jax
import jax.numpy as jnp
from jax import lax
from jax.experimental import pallas as pl
from jax.experimental.pallas import tpu as pltpu
from jax.sharding import PartitionSpec as P

TILE = 128
MESH = pl.DeviceIdType.MESH
SKEW = 2


def gather_kernel(dims, f_ref, a_ref, b_ref, recv_a, recv_b, send_z, send_p, send_b, send_f, local_a, local_b):
    levels, wide, high, cores, chunks = dims
    rows, width = f_ref.shape
    narrow = width // cores
    h = rows // chunks
    r, c = lax.axis_index("row"), lax.axis_index("col")
    k, z = lax.rem(r, cores), r // cores
    x, y = lax.rem(c, wide), c // wide
    x0, y0 = lax.rem(z, wide), z // wide
    source = c == z

    def chunk_rows(block, j):
        return pl.ds(pl.multiple_of(block * rows + j * h, h), h)

    def remote(src, dst, send, recv, row, col):
        return pltpu.make_async_remote_copy(
            src_ref=src, dst_ref=dst, send_sem=send, recv_sem=recv,
            device_id=(row, col), device_id_type=MESH,
        )

    def copies(t, j):
        m = z + t
        inside = m < levels
        has = inside & (m >= c)
        block = m * cores + k
        at = chunk_rows(block, j)
        if t == 0:
            def src(cols):
                return f_ref.at[pl.ds(j * h, h), cols]
        else:
            def src(cols):
                return a_ref.at[at, cols]
        everything = pl.ds(0, width)
        found = []
        for kk in range(cores):
            piece = src(pl.ds(kk * narrow, narrow))
            into = b_ref.at[at, :]
            for dx in range(1, wide):
                xt = lax.rem(x + dx, wide)
                found.append((
                    source & inside & (m >= y * wide + xt),
                    remote(piece, into, send_b.at[kk, dx, t, j], recv_b.at[block, j],
                           z * cores + kk, y * wide + xt),
                    False,
                ))
            for dy in range(1, high):
                yt = lax.rem(y + dy, high)
                found.append((
                    source & inside & (m >= yt * wide),
                    remote(piece, into, send_b.at[kk, wide - 1 + dy, t, j], recv_b.at[block, j],
                           z * cores + kk, yt * wide + x),
                    False,
                ))
        found.append((
            has & (z > 0),
            remote(src(everything), a_ref.at[at, :], send_z.at[t, j], recv_a.at[block, j],
                   r - cores, c),
            False,
        ))
        for dk in range(1, cores):
            other = z * cores + lax.rem(k + dk, cores)
            found.append((
                has,
                remote(src(everything), a_ref.at[at, :], send_p.at[dk, t, j], recv_a.at[block, j], other, c),
                False,
            ))
        for kk in range(cores):
            piece = src(pl.ds(kk * narrow, narrow))
            into = b_ref.at[at, :]
            found.append((
                source & inside & (k != kk),
                remote(piece, into, send_b.at[kk, 0, t, j], recv_b.at[block, j], z * cores + kk, c),
                False,
            ))
            found.append((
                source & inside & (k == kk),
                pltpu.make_async_copy(piece, into, local_b.at[t, j]),
                True,
            ))
        if t == 0:
            found.append((has, pltpu.make_async_copy(src(everything), a_ref.at[at, :], local_a.at[j]), True))
        return found

    def forwards(t, j, p):
        m = z + t
        block = m * cores + p
        part = b_ref.at[chunk_rows(block, j), :]
        mine = (x == x0) & (y != y0) & (m < levels)
        found = []
        for dx in range(1, wide):
            xt = lax.rem(x + dx, wide)
            found.append((
                mine & (m >= y * wide + xt),
                remote(part, part, send_f.at[dx, p, t, j], recv_b.at[block, j], r, y * wide + xt),
            ))
        return mine & (m >= y * wide), found

    def arrived(ref, sem):
        remote(ref, ref, send_z.at[0, 0], sem, r, c).wait_recv()

    def step(t, j):
        m = z + t
        block = m * cores + k
        if t > 0:
            @pl.when((m < levels) & (m >= c))
            def _():
                arrived(a_ref.at[chunk_rows(block, j), :], recv_a.at[block, j])
        for condition, copy, _ in copies(t, j):
            pl.when(condition)(copy.start)

    def forward(t, j):
        for p in range(cores):
            due, found = forwards(t, j, p)
            block = (z + t) * cores + p

            @pl.when(due)
            def _():
                arrived(b_ref.at[chunk_rows(block, j), :], recv_b.at[block, j])
            for condition, copy in found:
                pl.when(condition)(copy.start)

    order = [(t, j) for t in range(levels) for j in range(chunks)]
    for n, (t, j) in enumerate(order):
        step(t, j)
        if n >= SKEW:
            forward(*order[n - SKEW])
    for t, j in order[len(order) - SKEW:]:
        forward(t, j)

    for t, j in order:
        m = z + t
        inside = m < levels
        for dk in range(1, cores):
            block = m * cores + lax.rem(k + dk, cores)

            @pl.when(inside & (m >= c))
            def _():
                arrived(a_ref.at[chunk_rows(block, j), :], recv_a.at[block, j])

            @pl.when(inside & source)
            def _():
                arrived(b_ref.at[chunk_rows(block, j), :], recv_b.at[block, j])
        for p in range(cores):
            block = m * cores + p

            @pl.when(inside & (x != x0) & (m >= c))
            def _():
                arrived(b_ref.at[chunk_rows(block, j), :], recv_b.at[block, j])
        for condition, copy, local in copies(t, j):
            pl.when(condition)(copy.wait if local else copy.wait_send)
        for p in range(cores):
            for condition, copy in forwards(t, j, p)[1]:
                pl.when(condition)(copy.wait_send)


def gather(factor, n_row, n_col):
    rows, width = factor.shape
    cores = n_row // n_col
    wide = next(w for w in range(math.isqrt(n_col), 0, -1) if n_col % w == 0)
    high = n_col // wide
    levels = n_col
    chunks = max(1, 32 // n_row)
    dma = pltpu.SemaphoreType.DMA
    whole = rows * n_row
    return pl.pallas_call(
        functools.partial(gather_kernel, (levels, wide, high, cores, chunks)),
        out_shape=(
            jax.ShapeDtypeStruct((whole, width), factor.dtype),
            jax.ShapeDtypeStruct((whole, width // cores), factor.dtype),
        ),
        in_specs=[pl.BlockSpec(memory_space=pl.ANY)],
        out_specs=(pl.BlockSpec(memory_space=pl.ANY), pl.BlockSpec(memory_space=pl.ANY)),
        scratch_shapes=[
            dma((n_row, chunks)),
            dma((n_row, chunks)),
            dma((levels, chunks)),
            dma((cores, levels, chunks)),
            dma((cores, wide + high, levels, chunks)),
            dma((wide, cores, levels, chunks)),
            dma((chunks,)),
            dma((levels, chunks)),
        ],
        compiler_params=pltpu.CompilerParams(has_side_effects=True),
        cost_estimate=pl.CostEstimate(flops=0, bytes_accessed=whole * width * 32, transcendentals=0),
    )(factor)


def exchange_kernel(n_col, part_ref, out_ref, send, recv):
    r, c = lax.axis_index("row"), lax.axis_index("col")
    depth = out_ref.shape[1]
    started = []
    for d in range(1, n_col):
        ct = lax.rem(c + d, n_col)
        copy = pltpu.make_async_remote_copy(
            src_ref=part_ref.at[pl.ds(pl.multiple_of(ct * depth, depth), depth), :],
            dst_ref=out_ref.at[d - 1],
            send_sem=send.at[d - 1],
            recv_sem=recv.at[d - 1],
            device_id=(r, ct),
            device_id_type=MESH,
        )
        copy.start()
        started.append(copy)
    for copy in started:
        copy.wait()


def exchange(part, n_col):
    total, width = part.shape
    dma = pltpu.SemaphoreType.DMA
    return pl.pallas_call(
        functools.partial(exchange_kernel, n_col),
        out_shape=jax.ShapeDtypeStruct((n_col - 1, total // n_col, width), part.dtype),
        in_specs=[pl.BlockSpec(memory_space=pl.ANY)],
        out_specs=pl.BlockSpec(memory_space=pl.ANY),
        scratch_shapes=[dma((n_col - 1,)), dma((n_col - 1,))],
        compiler_params=pltpu.CompilerParams(has_side_effects=True),
    )(part)


def body(n_row, n_col, factor, sel_tiles, coupling):
    rows_here = factor.shape[0]
    row_index, col_index = lax.axis_index("row"), lax.axis_index("col")
    cores = n_row // n_col
    below, partner = gather(factor, n_row, n_col)
    coupling_full = lax.all_gather(coupling, "row", axis=1, tiled=True)

    def product(level, below, partner):
        first = level * rows_here * cores
        return lax.dot_general(
            partner[first:], below[first:], (((0,), (0,)), ((), ())), preferred_element_type=jnp.float32
        )

    gram = lax.switch(
        jnp.maximum(row_index // cores, col_index),
        [functools.partial(product, level) for level in range(n_col)],
        below,
        partner,
    )
    rounded = gram.astype(jnp.bfloat16)
    global_rows = row_index * rows_here + jnp.arange(rows_here, dtype=jnp.int32)
    member = jnp.any((global_rows // TILE)[:, None] == sel_tiles[None, :], axis=1)
    part = lax.dot_general(
        coupling_full, rounded, (((0,), (1,)), ((), ())), preferred_element_type=jnp.float32
    ).astype(jnp.bfloat16)
    depth = part.shape[0] // n_col
    arrived = exchange(part, n_col)
    summed = lax.dynamic_slice_in_dim(part, col_index * depth, depth, 0).astype(jnp.float32)
    for d in range(n_col - 1):
        summed = summed + arrived[d].astype(jnp.float32)
    child = jnp.where(member[None, :], -summed, jnp.float32(0.0))
    return (gram, child)


def solution(mesh):
    placed = (P("row", "col"), P(), P("col", "row"))
    return jax.shard_map(
        functools.partial(body, mesh.shape["row"], mesh.shape["col"]),
        mesh=mesh,
        in_specs=placed,
        out_specs=(P("row", "col"), P("col", "row")),
        check_vma=False,
    )
```

time: 818 us -> 520 us (0.64)
  waiting for transfers between devices: 724 us -> 0.7 us
  Pallas kernels: 0 us -> 441 us
  other arithmetic: 17 us -> 4.5 us
    pallas_call x0 -> x2, Pallas kernels: none -> 441 us  [the longest x1 392 us: gather(): pl.pallas_call(functools.partial(gather_kernel, (levels, wide, high, core...]
    psum x1 -> x0, waiting for transfers between devices: 305 us -> none  [from_root(): return lax.psum(kept, axis)]
    all_gather x1 -> x0, waiting for transfers between devices: 293 us -> none  [body(): whole = lax.all_gather(factor, 'row', axis=0, tiled=True)]
    reduce_scatter x1 -> x0, waiting for transfers between devices: 83.9 us -> none  [body(): lax.psum_scatter(lax.dot_general(coupling_full, rounded, (((0,), (1,)), (...]
    all_gather x1, waiting for transfers between devices: 41.2 us -> 0.02 us  [body(): coupling_full = lax.all_gather(coupling, 'row', axis=1, tiled=True)]
    select_n x1 -> x0, other arithmetic: 15 us -> none  [from_root(): jnp.where(lax.axis_index(axis) == source, value, 0).astype(value.dtype)]
  transfers between devices with their start and end apart: 4 -> 1, of which waited for: 4 -> 0; matrix products, arithmetic and copies ran while one was open for 5% -> 8% of each run, Pallas kernels for 0% -> 76%
where the time goes in v1:
time: 520 us; the launch traced here: 519 us
  Pallas kernels  441 us (85%)
  matrix products  59.1 us (11%)
  between operations  14.1 us (3%)
    pallas_call x1, Pallas kernels, gather(): pl.pallas_call(functools.partial(gather_kernel, (levels, wide, high, core...  392 us
    pallas_call x1, Pallas kernels, exchange(): pl.pallas_call(functools.partial(exchange_kernel, n_col), out_shape=jax.S...  48.6 us
    dot_general x1, matrix products, product(): lax.dot_general(partner[first:], below[first:], (((0,), (0,)), ((), ())),...  43.9 us
    dot_general x1, matrix products, body(): lax.dot_general(coupling_full, rounded, (((0,), (1,)), ((), ())), preferr...  15.1 us
  transfers between devices with their start and end apart: 1, of which 0 were waited for; matrix products, arithmetic and copies ran while one was open for 8% of the time, Pallas kernels for 76%

profile of v1, /device:TPU:0, one launch (start us, length us, event | category | flops | bytes accessed | tf_op | source)
XLA Modules:
  0.0 519.4 jit_solution(11622441116960088934)
XLA Ops:
  7.2 0.0 all-gather.2.cloned.1.call-start
  7.2 0.7 all-gather.2.cloned.1.call-update
  7.9 392.4 %shard_map.50 = (bf16[8192,2048]{1,0:T(8,128)(2,1)}, bf16[8192,1024]{1,0:T(8,128)(2,1)}) custom-call(bf16[1024,2048]{1,0:T(8,128)(2,1)} %f_ref.1), custom_call_target="tpu_custom_call" | custom-call | bytes 536870912 | tf_op jit(solution)/shard_map/pallas_call | solution.py:180
  400.3 0.0 copy-start
  400.3 44.0 %conditional.1 = (f32[1024,2048]{1,0:T(8,128)}) conditional(s32[]{:T(128)} %clamp.3, (bf16[8192,1024]{1,0:T(8,128)(2,1)}, bf16[8192,2048]{1,0:T(8,128)(2,1)}) %tuple.20, (bf16[8192,1024]{1,0:T(8,128)(2,1)}, bf16[8192,2048]{1,0:T(8,128)(2,1)}) %tuple.20, (bf16[8192,1024]{1,0:T(8,128)(2,1)}, ...), branch_computations={%region_0.1_spmd, %region_1.2_spmd, %region_2.3_spmd, %region_3.4_... | conditional | flops 34359738368 | bytes 58720264 | solution.py:249
  400.4 43.9 %fusion.19 = f32[1024,2048]{1,0:T(8,128)} fusion(bf16[8192,1024]{1,0:T(8,128)(2,1)} %get-tuple-element.18, bf16[8192,2048]{1,0:T(8,128)(2,1)} %get-tuple-element.19), kind=kOutput, calls=%fused_computation.27 | convolution fusion | flops 34359738368 | bytes 58720256 | tf_op jit(solution)/shard_map/cond/branch_0_fun/dot_general | solution.py:245
  444.3 0.0 copy-done
  444.3 0.1 compare_reduce_fusion
  444.4 0.0 all-gather.2.cloned.1.call-done
  444.5 15.1 %fusion.11 = bf16[1024,2048]{0,1:T(8,128)(2,1)} fusion(bf16[2048,2048]{1,0:T(8,128)(2,1)} %all-gather.2.cloned.1.call-done, f32[1024,2048]{1,0:T(8,128)} %get-tuple-element.35), kind=kOutput, calls=%fused_computation.11 | convolution fusion | flops 8594128896 | bytes 20971520 | tf_op jit(solution)/shard_map/dot_general | solution.py:258
  459.6 48.6 %shard_map.51 = bf16[3,512,1024]{2,1,0:T(8,128)(2,1)} custom-call(bf16[2048,1024]{1,0:T(8,128)(2,1)} %bitcast.15), custom_call_target="tpu_custom_call" | custom-call | tf_op jit(solution)/shard_map/pallas_call | solution.py:226
  508.2 4.4 fusion.15
  (1 shorter events, 0.0 us)
Async XLA Ops:
  7.2 437.3 %all-gather.2.cloned.1.call-start = ((), (), s32[]{:S(2)}) async-start(), calls=%async_computation | async-start | bytes 9437184 | tf_op jit(solution)/shard_map/all_gather | solution.py:241
  400.3 44.0 %copy-start = (s32[32]{0:T(128)S(1)}, s32[32]{0:T(128)}, u32[]{:S(2)}) copy-start(s32[32]{0:T(128)} %param.8) | copy-start | bytes 388
Sparse Core Ops, SparseCore 0:
  9.6 142.3 all-gather.1

commit v2 on v1

--- a/solution.py
+++ b/solution.py
@@ -13,7 +13,7 @@
 SKEW = 2
 
 
-def gather_kernel(dims, f_ref, a_ref, b_ref, recv_a, recv_b, send_z, send_p, send_b, send_f, local_a, local_b):
+def gather_kernel(dims, f_ref, a_ref, b_ref, recv_a, recv_b, send_z, send_p, send_b, send_f, local_a, stage):
     levels, wide, high, cores, chunks = dims
     rows, width = f_ref.shape
     narrow = width // cores
@@ -87,14 +87,31 @@
                 remote(piece, into, send_b.at[kk, 0, t, j], recv_b.at[block, j], z * cores + kk, c),
                 False,
             ))
-            found.append((
-                source & inside & (k == kk),
-                pltpu.make_async_copy(piece, into, local_b.at[t, j]),
-                True,
-            ))
-        if t == 0:
-            found.append((has, pltpu.make_async_copy(src(everything), a_ref.at[at, :], local_a.at[j]), True))
         return found
+
+    def keep(t, j):
+        m = z + t
+        at = chunk_rows(m * cores + k, j)
+        here = f_ref.at[pl.ds(j * h, h), :] if t == 0 else a_ref.at[at, :]
+        inside = (m < levels) & (m >= c)
+
+        @pl.when(inside if t == 0 else inside & source)
+        def _():
+            load = pltpu.make_async_copy(here, stage, local_a.at[0])
+            load.start()
+            load.wait()
+            if t == 0:
+                pltpu.make_async_copy(stage, a_ref.at[at, :], local_a.at[1]).start()
+            for kk in range(cores):
+                @pl.when(source & (k == kk))
+                def _():
+                    store = pltpu.make_async_copy(
+                        stage.at[:, pl.ds(kk * narrow, narrow)], b_ref.at[at, :], local_a.at[2]
+                    )
+                    store.start()
+                    store.wait()
+            if t == 0:
+                pltpu.make_async_copy(stage, a_ref.at[at, :], local_a.at[1]).wait()
 
     def forwards(t, j, p):
         m = z + t
@@ -122,6 +139,7 @@
                 arrived(a_ref.at[chunk_rows(block, j), :], recv_a.at[block, j])
         for condition, copy, _ in copies(t, j):
             pl.when(condition)(copy.start)
+        keep(t, j)
 
     def forward(t, j):
         for p in range(cores):
@@ -192,8 +210,8 @@
             dma((cores, levels, chunks)),
             dma((cores, wide + high, levels, chunks)),
             dma((wide, cores, levels, chunks)),
-            dma((chunks,)),
-            dma((levels, chunks)),
+            dma((3,)),
+            pltpu.VMEM((rows // chunks, width), factor.dtype),
         ],
         compiler_params=pltpu.CompilerParams(has_side_effects=True),
         cost_estimate=pl.CostEstimate(flops=0, bytes_accessed=whole * width * 32, transcendentals=0),

time: 520 us -> 500 us (0.962)
  Pallas kernels: 441 us -> 421 us
    pallas_call x1, Pallas kernels: 392 us -> 373 us  [gather(): pl.pallas_call(functools.partial(gather_kernel, (levels, wide, high, core...]
  transfers between devices with their start and end apart: 1 -> 1, of which waited for: 0 -> 0; matrix products, arithmetic and copies ran while one was open for 8% -> 9% of each run, Pallas kernels for 76% -> 75%
where the time goes in v2:
time: 500 us
  Pallas kernels  421 us (84%)
  matrix products  59.1 us (12%)
  between operations  14.1 us (3%)
    pallas_call x1, Pallas kernels, gather(): pl.pallas_call(functools.partial(gather_kernel, (levels, wide, high, core...  373 us
    pallas_call x1, Pallas kernels, exchange(): pl.pallas_call(functools.partial(exchange_kernel, n_col), out_shape=jax.S...  48.3 us
    dot_general x1, matrix products, product(): lax.dot_general(partner[first:], below[first:], (((0,), (0,)), ((), ())),...  43.9 us
    dot_general x1, matrix products, body(): lax.dot_general(coupling_full, rounded, (((0,), (1,)), ((), ())), preferr...  15.1 us
  transfers between devices with their start and end apart: 1, of which 0 were waited for; matrix products, arithmetic and copies ran while one was open for 9% of the time, Pallas kernels for 75%

profile of v2, /device:TPU:0, one launch (start us, length us, event | category | flops | bytes accessed | tf_op | source)
XLA Modules:
  0.0 499.6 jit_solution(5893461267527661360)
XLA Ops:
  7.2 0.0 all-gather.2.cloned.1.call-start
  7.2 0.7 all-gather.2.cloned.1.call-update
  7.9 372.9 %shard_map.50 = (bf16[8192,2048]{1,0:T(8,128)(2,1)}, bf16[8192,1024]{1,0:T(8,128)(2,1)}) custom-call(bf16[1024,2048]{1,0:T(8,128)(2,1)} %f_ref.1), custom_call_target="tpu_custom_call" | custom-call | bytes 536870912 | tf_op jit(solution)/shard_map/pallas_call | solution.py:198
  380.8 0.0 copy-start
  380.8 44.0 %conditional.1 = (f32[1024,2048]{1,0:T(8,128)}) conditional(s32[]{:T(128)} %clamp.3, (bf16[8192,1024]{1,0:T(8,128)(2,1)}, bf16[8192,2048]{1,0:T(8,128)(2,1)}) %tuple.20, (bf16[8192,1024]{1,0:T(8,128)(2,1)}, bf16[8192,2048]{1,0:T(8,128)(2,1)}) %tuple.20, (bf16[8192,1024]{1,0:T(8,128)(2,1)}, ...), branch_computations={%region_0.1_spmd, %region_1.2_spmd, %region_2.3_spmd, %region_3.4_... | conditional | flops 34359738368 | bytes 58720264 | solution.py:267
  380.8 43.9 %fusion.19 = f32[1024,2048]{1,0:T(8,128)} fusion(bf16[8192,1024]{1,0:T(8,128)(2,1)} %get-tuple-element.18, bf16[8192,2048]{1,0:T(8,128)(2,1)} %get-tuple-element.19), kind=kOutput, calls=%fused_computation.27 | convolution fusion | flops 34359738368 | bytes 58720256 | tf_op jit(solution)/shard_map/cond/branch_0_fun/dot_general | solution.py:263
  424.8 0.0 copy-done
  424.8 0.1 compare_reduce_fusion
  424.9 0.0 all-gather.2.cloned.1.call-done
  424.9 15.1 %fusion.11 = bf16[1024,2048]{0,1:T(8,128)(2,1)} fusion(bf16[2048,2048]{1,0:T(8,128)(2,1)} %all-gather.2.cloned.1.call-done, f32[1024,2048]{1,0:T(8,128)} %get-tuple-element.35), kind=kOutput, calls=%fused_computation.11 | convolution fusion | flops 8594128896 | bytes 20971520 | tf_op jit(solution)/shard_map/dot_general | solution.py:276
  440.0 48.3 %shard_map.51 = bf16[3,512,1024]{2,1,0:T(8,128)(2,1)} custom-call(bf16[2048,1024]{1,0:T(8,128)(2,1)} %bitcast.15), custom_call_target="tpu_custom_call" | custom-call | tf_op jit(solution)/shard_map/pallas_call | solution.py:244
  488.4 4.4 fusion.15
  (1 shorter events, 0.0 us)
Async XLA Ops:
  7.2 417.7 %all-gather.2.cloned.1.call-start = ((), (), s32[]{:S(2)}) async-start(), calls=%async_computation | async-start | bytes 9437184 | tf_op jit(solution)/shard_map/all_gather | solution.py:259
  380.8 44.0 %copy-start = (s32[32]{0:T(128)S(1)}, s32[32]{0:T(128)}, u32[]{:S(2)}) copy-start(s32[32]{0:T(128)} %param.8) | copy-start | bytes 388
Sparse Core Ops, SparseCore 0:
  9.6 142.3 all-gather.1
